TPU v7x, 32 devices: a whole 2x2x4 slice. The times are simulated.
32 devices in a mesh: owner: 4 (over y, x), rows: 8 (over z, core).
Axes of the slice: x: 2, y: 2, z: 4, core: 2. Of those that a mesh axis runs over, the one named last changes fastest.
Arguments:
- w_gate: float32 [64, 2048, 1024], P('owner', 'rows'), may hold values from -0.1875 to 0.1875
- avg_gate: bfloat16 [64, 2048, 1024], P('owner', 'rows'), may hold values from -0.0625 to 0.0625
- w_up: float32 [64, 2048, 1024], P('owner', 'rows'), may hold values from -0.1875 to 0.1875
- avg_up: bfloat16 [64, 2048, 1024], P('owner', 'rows'), may hold values from -0.0625 to 0.0625
- w_down: float32 [64, 1024, 2048], P('owner', None, 'rows'), may hold values from -0.25 to 0.25
- avg_down: bfloat16 [64, 1024, 2048], P('owner', None, 'rows'), may hold values from -0.09375 to 0.09375
- router_weight: float32 [2048, 64], P('rows', 'owner'), may hold values from -0.125 to 0.125
- router_gain: float32 [2048], P('rows'), may hold values from 0.25 to 1.75
Outputs:
- serve_gate: bfloat16 [64, 2048, 1024], P('owner', None, 'rows')
- serve_up: bfloat16 [64, 2048, 1024], P('owner', None, 'rows')
- serve_down: bfloat16 [64, 1024, 2048], P('owner', 'rows')
- scale_gate: float32 [64, 1024], P('owner', 'rows')
- scale_up: float32 [64, 1024], P('owner', 'rows')
- scale_down: float32 [64, 1024], P('owner', 'rows')
- serve_router: bfloat16 [2048, 64], replicated
All inputs are finite; a program needn't handle non-finite values.
Results may differ from a plain program's by a relative error of at most 0.0015.
Values may be sent and summed in bfloat16 or wider, within the bound.
A program may use at most 192 MiB of HBM per device.

v0:
```python
import jax
import jax.numpy as jnp
from jax import lax
from jax.sharding import PartitionSpec as P


def shards(w_gate, avg_gate, w_up, avg_up, w_down, avg_down, router_weight, router_gain):
    fresh_gate = w_gate + avg_gate.astype(jnp.float32)
    fresh_up = w_up + avg_up.astype(jnp.float32)
    fresh_down = w_down + avg_down.astype(jnp.float32)
    total_gate, total_up, total_down = lax.psum(
        (
            jnp.sum(fresh_gate * fresh_gate, axis=1),
            jnp.sum(fresh_up * fresh_up, axis=1),
            jnp.sum(fresh_down * fresh_down, axis=2),
        ),
        "rows",
    )
    scale_gate = jnp.sqrt(total_gate)
    scale_up = jnp.sqrt(total_up)
    scale_down = jnp.sqrt(total_down)
    narrow_gate, narrow_up, narrow_down = (
        (fresh_gate / jnp.expand_dims(scale_gate, 1)).astype(jnp.bfloat16),
        (fresh_up / jnp.expand_dims(scale_up, 1)).astype(jnp.bfloat16),
        (fresh_down / jnp.expand_dims(scale_down, 2)).astype(jnp.bfloat16),
    )
    serve_gate, serve_up = (
        lax.all_to_all(narrow_gate, "rows", split_axis=2, concat_axis=1, tiled=True),
        lax.all_to_all(narrow_up, "rows", split_axis=2, concat_axis=1, tiled=True),
    )
    serve_down = lax.all_to_all(narrow_down, "rows", split_axis=1, concat_axis=2, tiled=True)
    scale_gate = lax.dynamic_slice_in_dim(
        scale_gate, lax.axis_index("rows") * serve_gate.shape[2], serve_gate.shape[2], axis=1
    )
    scale_up = lax.dynamic_slice_in_dim(
        scale_up, lax.axis_index("rows") * serve_up.shape[2], serve_up.shape[2], axis=1
    )
    scale_down = lax.dynamic_slice_in_dim(
        scale_down, lax.axis_index("rows") * serve_down.shape[1], serve_down.shape[1], axis=1
    )
    part_router = (router_weight * router_gain[:, None]).astype(jnp.bfloat16)
    row_router = lax.all_gather(part_router, "rows", axis=0, tiled=True)
    serve_router = lax.all_gather(row_router, "owner", axis=1, tiled=True)
    return (serve_gate, serve_up, serve_down, scale_gate, scale_up, scale_down, serve_router)


def solution(mesh):
    return jax.shard_map(
        shards,
        mesh=mesh,
        in_specs=(
            P("owner", "rows", None),
            P("owner", "rows", None),
            P("owner", "rows", None),
            P("owner", "rows", None),
            P("owner", None, "rows"),
            P("owner", None, "rows"),
            P("rows", "owner"),
            P("rows"),
        ),
        out_specs=(
            P("owner", None, "rows"),
            P("owner", None, "rows"),
            P("owner", "rows", None),
            P("owner", "rows"),
            P("owner", "rows"),
            P("owner", "rows"),
            P(),
        ),
        check_vma=False,
    )
```

profile of v0, /device:TPU:0, one launch (start us, length us, event | category | flops | bytes accessed | tf_op | source)
XLA Modules:
  0.0 824.8 jit_solution(4685212397091970850)
XLA Ops:
  7.2 0.0 all-reduce.3.cloned.1.call-start
  7.2 17.6 %copy.31 = f32[16,256,1024]{1,0,2:T(8,128)} copy(f32[16,256,1024]{2,1,0:T(8,128)} %param.8) | data formatting | bytes 33554432 | tf_op args[0]
  24.8 17.6 %copy.34 = f32[16,256,1024]{1,0,2:T(8,128)} copy(f32[16,256,1024]{2,1,0:T(8,128)} %param.10) | data formatting | bytes 33554432 | tf_op args[2]
  42.4 12.5 %copy.30 = bf16[16,256,1024]{1,0,2:T(8,128)(2,1)} copy(bf16[16,256,1024]{2,1,0:T(8,128)(2,1)} %param.9) | data formatting | bytes 16777216 | tf_op args[1]
  54.9 12.5 %copy.33 = bf16[16,256,1024]{1,0,2:T(8,128)(2,1)} copy(bf16[16,256,1024]{2,1,0:T(8,128)(2,1)} %param.11) | data formatting | bytes 16777216 | tf_op args[3]
  67.4 0.0 copy-start
  67.4 0.0 copy-start.1
  67.4 25.2 %multiply_reduce_fusion = f32[16,1024]{0,1:T(8,128)} fusion(f32[16,1024,256]{2,1,0:T(8,128)} %param.12, bf16[16,1024,256]{2,1,0:T(8,128)(2,1)} %param.13), kind=kLoop, calls=%fused_computation.2 | loop fusion | flops 16760832 | bytes 25231360 | tf_op jit(solution)/shard_map/reduce_sum | solution.py:15
  92.6 0.0 copy-done
  92.6 0.0 copy-done.1
  92.6 13.2 %multiply_reduce_fusion.1 = (f32[16,1024]{0,1:T(8,128)}, f32[16,1024]{0,1:T(8,128)}) fusion(f32[16,256,1024]{1,0,2:T(8,128)} %copy.34, bf16[16,256,1024]{1,0,2:T(8,128)(2,1)S(1)} %copy-done.1, f32[16,256,1024]{1,0,2:T(8,128)} %copy.31, bf16[16,256,1024]{1,0,2:T(8,128)(2,1)S(1)} %copy-done), kind=kLoop, calls=%fused_computation.4 | loop fusion | flops 33521664 | bytes 50462720 | tf_op jit(solution)/shard_map/reduce_sum | solution.py:14
  105.8 0.0 all-reduce.3.cloned.1.call-update
  105.8 65.1 %all-reduce.3.cloned.1.call-done = (f32[16,1024]{0,1:T(8,128)}, f32[16,1024]{0,1:T(8,128)}, f32[16,1024]{0,1:T(8,128)}) async-done(((f32[16,1024]{0,1:T(8,128)}, f32[16,1024]{0,1:T(8,128)}, f32[16,1024]{0,1:T(8,128)}), (f32[16,1024]{0,1:T(8,128)}, f32[16,1024]{0,1:T(8,128)}, f32[16,1024]{0,1:T(8,128)})) %all-reduce.3.cloned.1.call-update) | async-done | bytes 196624 | tf_op jit(solution)/shard_map/psum | solution.py:11
  170.9 1.2 sqrt.10
  172.1 12.0 %divide_convert_fusion.1 = bf16[16,256,1024]{1,0,2:T(8,128)(2,1)} fusion(f32[16,256,1024]{1,0,2:T(8,128)} %copy.34, bf16[16,256,1024]{1,0,2:T(8,128)(2,1)} %copy.33, f32[16,1024]{0,1:T(8,128)S(1)} %sqrt.10), kind=kLoop, calls=%fused_computation.3 | loop fusion | flops 16777216 | bytes 33619968 | tf_op jit(solution)/shard_map/convert_element_type | solution.py:24
  184.1 0.0 copy-start.3
  184.1 5.1 all-to-all-start.1
  189.2 0.0 copy-done.3
  189.2 0.1 sqrt.9
  189.3 12.0 %divide_convert_fusion.2 = bf16[16,256,1024]{1,0,2:T(8,128)(2,1)} fusion(f32[16,256,1024]{1,0,2:T(8,128)} %copy.31, bf16[16,256,1024]{1,0,2:T(8,128)(2,1)} %copy.30, f32[16,1024]{0,1:T(8,128)S(1)} %sqrt.9), kind=kLoop, calls=%fused_computation.6 | loop fusion | flops 16777216 | bytes 33619968 | tf_op jit(solution)/shard_map/convert_element_type | solution.py:23
  201.3 0.0 copy-start.2
  201.3 171.7 %all-to-all-done.1 = bf16[16,256,1024]{1,0,2:T(8,128)(2,1)} async-done(((bf16[16,256,1024]{1,0,2:T(8,128)(2,1)}), bf16[16,256,1024]{1,0,2:T(8,128)(2,1)}, u32[]{:S(2)}, u32[]{:S(2)}) %all-to-all-start.1) | async-done | bytes 8388640 | tf_op jit(solution)/shard_map/all_to_all | solution.py:29
  373.0 5.1 all-to-all-start
  378.2 0.0 copy-done.2
  378.2 0.1 sqrt.11
  378.3 23.8 %divide_convert_fusion = bf16[16,1024,256]{2,0,1:T(8,128)(2,1)} fusion(f32[16,1024,256]{2,1,0:T(8,128)} %param.12, f32[16,1024]{0,1:T(8,128)S(1)} %sqrt.11, bf16[16,1024,256]{2,1,0:T(8,128)(2,1)} %param.13), kind=kLoop, calls=%fused_computation.1 | loop fusion | flops 16777216 | bytes 33619968 | tf_op jit(solution)/shard_map/convert_element_type | solution.py:25
  402.1 0.0 copy-start.4
  402.1 0.0 copy-start.5
  402.1 159.8 %all-to-all-done = bf16[16,256,1024]{1,0,2:T(8,128)(2,1)} async-done(((bf16[16,256,1024]{1,0,2:T(8,128)(2,1)}), bf16[16,256,1024]{1,0,2:T(8,128)(2,1)}, u32[]{:S(2)}, u32[]{:S(2)}) %all-to-all-start) | async-done | bytes 8388640 | tf_op jit(solution)/shard_map/all_to_all | solution.py:28
  561.8 5.0 all-to-all-start.2
  566.9 0.0 copy-done.4
  566.9 0.0 copy-done.5
  566.9 189.9 %all_gather.6 = bf16[2048,16]{0,1:T(8,128)(2,1)S(1)} all-gather(bf16[256,16]{0,1:T(8,128)(2,1)S(1)} %multiply_convert_fusion), channel_id=1, replica_groups=mesh['owner'=4,'rows'=8] {'rows'}, dimensions={0}, use_global_device_ids=true | all-gather | bytes 73728 | tf_op jit(solution)/shard_map/all_gather | solution.py:42
  756.8 9.1 %all_gather.7 = bf16[2048,64]{0,1:T(8,128)(2,1)S(1)} all-gather(bf16[2048,16]{0,1:T(8,128)(2,1)S(1)} %all_gather.6), channel_id=1, replica_groups=mesh['owner'=4,'rows'=8] {'owner'}, dimensions={1}, use_global_device_ids=true | all-gather | bytes 327680 | tf_op jit(solution)/shard_map/all_gather | solution.py:43
  765.9 0.7 copy.39
  766.6 0.7 copy.40
  767.3 0.7 copy.41
  767.9 12.3 %copy.35 = bf16[16,8,256,128]{3,2,1,0:T(8,128)(2,1)} copy(bf16[16,8,256,128]{2,0,3,1:T(8,128)(2,1)} %bitcast.4) | data formatting | bytes 16777216 | tf_op jit(solution)/shard_map/all_to_all | solution.py:29
  780.2 12.3 %copy.32 = bf16[16,8,256,128]{3,2,1,0:T(8,128)(2,1)} copy(bf16[16,8,256,128]{2,0,3,1:T(8,128)(2,1)} %bitcast.1) | data formatting | bytes 16777216 | tf_op jit(solution)/shard_map/all_to_all | solution.py:28
  792.5 0.0 all-to-all-done.2
  792.5 11.4 %copy.38 = bf16[16,128,8,256]{3,2,1,0:T(8,128)(2,1)} copy(bf16[16,128,8,256]{3,0,1,2:T(8,128)(2,1)} %bitcast.7) | data formatting | bytes 16777216 | tf_op jit(solution)/shard_map/all_to_all | solution.py:31
  803.9 13.4 %all_to_all.50 = bf16[16,128,2048]{2,1,0:T(8,128)(2,1)} reshape(bf16[16,128,8,256]{3,2,1,0:T(8,128)(2,1)} %copy.38) | data formatting | bytes 16777216 | tf_op jit(solution)/shard_map/all_to_all | solution.py:31
  817.3 0.7 copy.53
  (4 shorter events, 0.0 us)
Async XLA Ops:
  7.2 163.7 %all-reduce.3.cloned.1.call-start = ((), (), s32[]{:S(2)}) async-start(), calls=%async_computation.3 | async-start | bytes 3145728 | tf_op jit(solution)/shard_map/psum | solution.py:11
  67.4 25.2 %copy-start = (bf16[16,256,1024]{1,0,2:T(8,128)(2,1)S(1)}, bf16[16,256,1024]{1,0,2:T(8,128)(2,1)}, u32[]{:S(2)}) copy-start(bf16[16,256,1024]{1,0,2:T(8,128)(2,1)} %copy.30) | copy-start | bytes 25165828
  67.4 25.2 %copy-start.1 = (bf16[16,256,1024]{1,0,2:T(8,128)(2,1)S(1)}, bf16[16,256,1024]{1,0,2:T(8,128)(2,1)}, u32[]{:S(2)}) copy-start(bf16[16,256,1024]{1,0,2:T(8,128)(2,1)} %copy.33) | copy-start | bytes 25165828
  184.1 5.1 copy-start.3
  184.1 189.0 %all-to-all-start.1 = ((bf16[16,256,1024]{1,0,2:T(8,128)(2,1)}), bf16[16,256,1024]{1,0,2:T(8,128)(2,1)}, u32[]{:S(2)}, u32[]{:S(2)}) async-start(bf16[16,256,1024]{1,0,2:T(8,128)(2,1)} %divide_convert_fusion.1), calls=%async_computation.1 | async-start | bytes 16777216 | tf_op jit(solution)/shard_map/all_to_all | solution.py:29
  201.3 176.9 %copy-start.2 = (f32[16,1024]{0,1:T(8,128)S(1)}, f32[16,1024]{0,1:T(8,128)}, u32[]{:S(2)}) copy-start(f32[16,1024]{0,1:T(8,128)} %get-tuple-element.16) | copy-start | bytes 196612
  373.0 188.8 %all-to-all-start = ((bf16[16,256,1024]{1,0,2:T(8,128)(2,1)}), bf16[16,256,1024]{1,0,2:T(8,128)(2,1)}, u32[]{:S(2)}, u32[]{:S(2)}) async-start(bf16[16,256,1024]{1,0,2:T(8,128)(2,1)} %divide_convert_fusion.2), calls=%async_computation | async-start | bytes 16777216 | tf_op jit(solution)/shard_map/all_to_all | solution.py:28
  402.1 164.8 %copy-start.4 = (f32[256,16]{0,1:T(8,128)S(1)}, f32[256,16]{0,1:T(8,128)}, u32[]{:S(2)}) copy-start(f32[256,16]{0,1:T(8,128)} %param.14) | copy-start | bytes 49156
  402.1 164.8 %copy-start.5 = (f32[256]{0:T(256)S(1)}, f32[256]{0:T(256)}, u32[]{:S(2)}) copy-start(f32[256]{0:T(256)} %param.15) | copy-start | bytes 3076
  561.8 230.7 %all-to-all-start.2 = ((bf16[16,1024,256]{2,0,1:T(8,128)(2,1)}), bf16[16,1024,256]{2,0,1:T(8,128)(2,1)}, u32[]{:S(2)}, u32[]{:S(2)}) async-start(bf16[16,1024,256]{2,0,1:T(8,128)(2,1)} %divide_convert_fusion), calls=%async_computation.2 | async-start | bytes 16777216 | tf_op jit(solution)/shard_map/all_to_all | solution.py:31
Sparse Core Ops, SparseCore 0:
  105.9 64.9 all-reduce.2
where the time goes:
time: 827 us; the launch traced here: 825 us
  waiting for transfers between devices  397 us (48%)
  blocking collectives  199 us (24%)
  local copies, waits for them, and re-layouts  114 us (14%)
  other arithmetic  86.1 us (10%)
  starting transfers between devices  15.3 us (2%)
  between operations  14.1 us (2%)
    all_gather x1, blocking collectives, shards(): row_router = lax.all_gather(part_router, 'rows', axis=0, tiled=True)  190 us
    all_to_all x1, waiting for transfers between devices, shards(): lax.all_to_all(narrow_up, 'rows', split_axis=2, concat_axis=1, tiled=True)  172 us
    all_to_all x1, waiting for transfers between devices, shards(): lax.all_to_all(narrow_gate, 'rows', split_axis=2, concat_axis=1, tiled=True)  160 us
    psum x1, waiting for transfers between devices, shards(): lax.psum((jnp.sum(fresh_gate * fresh_gate, axis=1), jnp.sum(fresh_up * fr...  65.1 us
    unnamed x20, local copies, waits for them, and re-layouts  62.9 us
    reduce_sum x1, other arithmetic, shards(): jnp.sum(fresh_down * fresh_down, axis=2)  25.2 us
    all_to_all x2, local copies, waits for them, and re-layouts, shards(): lax.all_to_all(narrow_down, 'rows', split_axis=1, concat_axis=2, tiled=True)  24.8 us
    convert_element_type x1, other arithmetic, shards(): (fresh_down / jnp.expand_dims(scale_down, 2)).astype(jnp.bfloat16)  23.8 us
  transfers between devices with their start and end apart: 4, of which 3 were waited for; matrix products, arithmetic and copies ran while one was open for 8% of the time, Pallas kernels for 0%

commit v1 on v0

--- a/solution.py
+++ b/solution.py
@@ -25,7 +25,12 @@
         (fresh_down / jnp.expand_dims(scale_down, 2)).astype(jnp.bfloat16),
     )
     serve_gate, serve_up = (
-        lax.all_to_all(narrow_gate, "rows", split_axis=2, concat_axis=1, tiled=True),
+        jnp.concatenate(
+            lax.all_to_all(
+                jnp.stack(jnp.split(narrow_gate, lax.axis_size("rows"), axis=2)), "rows", 0, 0
+            ),
+            axis=1,
+        ),
         lax.all_to_all(narrow_up, "rows", split_axis=2, concat_axis=1, tiled=True),
     )
     serve_down = lax.all_to_all(narrow_down, "rows", split_axis=1, concat_axis=2, tiled=True)

time: 827 us -> 791 us (0.956)
  local copies, waits for them, and re-layouts: 114 us -> 89 us
  waiting for transfers between devices: 397 us -> 387 us
    all_to_all x1, waiting for transfers between devices: 0.01 us -> 164 us  [shards(): lax.all_to_all(narrow_down, 'rows', split_axis=1, concat_axis=2, tiled=True)]
    all_to_all x1, waiting for transfers between devices: 160 us -> 0.01 us  [shards(): lax.all_to_all(jnp.stack(jnp.split(narrow_gate, lax.axis_size('rows'), ax...]
    unnamed x20 -> x34, local copies, waits for them, and re-layouts: 62.9 us -> 40.9 us
    all_to_all x1 -> x0, local copies, waits for them, and re-layouts: 12.3 us -> none  [shards(): lax.all_to_all(narrow_gate, 'rows', split_axis=2, concat_axis=1, tiled=True)]
    all_to_all x1, waiting for transfers between devices: 172 us -> 160 us  [shards(): lax.all_to_all(narrow_up, 'rows', split_axis=2, concat_axis=1, tiled=True)]
    reduce_sum x0 -> x1, other arithmetic: none -> 10.6 us  [shards(): jnp.sum(fresh_gate * fresh_gate, axis=1)]
    reduce_sum x1, other arithmetic: 13.2 us -> 4.34 us  [shards(): jnp.sum(fresh_up * fresh_up, axis=1)]
  transfers between devices with their start and end apart: 4 -> 4, of which waited for: 3 -> 3; matrix products, arithmetic and copies ran while one was open for 8% -> 9% of each run, Pallas kernels for 0% -> 0%
where the time goes in v1:
time: 791 us; the launch traced here: 789 us
  waiting for transfers between devices  387 us (49%)
  blocking collectives  199 us (25%)
  local copies, waits for them, and re-layouts  89 us (11%)
  other arithmetic  84.7 us (11%)
  starting transfers between devices  15.3 us (2%)
  between operations  14.2 us (2%)
    all_gather x1, blocking collectives, shards(): row_router = lax.all_gather(part_router, 'rows', axis=0, tiled=True)  190 us
    all_to_all x1, waiting for transfers between devices, shards(): lax.all_to_all(narrow_down, 'rows', split_axis=1, concat_axis=2, tiled=True)  164 us
    all_to_all x1, waiting for transfers between devices, shards(): lax.all_to_all(narrow_up, 'rows', split_axis=2, concat_axis=1, tiled=True)  160 us
    psum x1, waiting for transfers between devices, shards(): lax.psum((jnp.sum(fresh_gate * fresh_gate, axis=1), jnp.sum(fresh_up * fr...  62.6 us
    unnamed x34, local copies, waits for them, and re-layouts  40.9 us
    all_to_all x2, local copies, waits for them, and re-layouts, shards(): lax.all_to_all(narrow_down, 'rows', split_axis=1, concat_axis=2, tiled=True)  24.8 us
    reduce_sum x1, other arithmetic, shards(): jnp.sum(fresh_down * fresh_down, axis=2)  24.6 us
    convert_element_type x1, other arithmetic, shards(): (fresh_down / jnp.expand_dims(scale_down, 2)).astype(jnp.bfloat16)  23.8 us
  transfers between devices with their start and end apart: 4, of which 3 were waited for; matrix products, arithmetic and copies ran while one was open for 9% of the time, Pallas kernels for 0%

profile of v1, /device:TPU:0, one launch (start us, length us, event | category | flops | bytes accessed | tf_op | source)
XLA Modules:
  0.0 789.0 jit_solution(4520369092743525560)
XLA Ops:
  7.2 0.0 all-reduce.3.cloned.1.call-start
  7.2 12.5 %copy.28 = bf16[16,256,1024]{1,0,2:T(8,128)(2,1)} copy(bf16[16,256,1024]{2,1,0:T(8,128)(2,1)} %param.11) | data formatting | bytes 16777216 | tf_op args[3]
  19.7 17.6 %copy.29 = f32[16,256,1024]{1,0,2:T(8,128)} copy(f32[16,256,1024]{2,1,0:T(8,128)} %param.10) | data formatting | bytes 33554432 | tf_op args[2]
  37.3 0.0 copy-start
  37.3 0.0 slice-start
  37.3 0.0 slice-start.1
  37.3 0.0 slice-start.4
  37.3 10.6 %multiply_reduce_fusion.2 = f32[16,1024]{1,0:T(8,128)} fusion(f32[16,256,1024]{2,1,0:T(8,128)} %param.8, bf16[16,256,1024]{2,1,0:T(8,128)(2,1)} %param.9), kind=kLoop, calls=%fused_computation.7 | loop fusion | flops 16760832 | bytes 25231360 | tf_op jit(solution)/shard_map/reduce_sum | solution.py:13
  47.9 0.0 copy-done
  47.9 0.0 slice-start.2
  47.9 0.0 slice-start.3
  47.9 0.0 slice-start.5
  47.9 24.6 %multiply_reduce_fusion = f32[16,1024]{0,1:T(8,128)} fusion(f32[16,1024,256]{2,1,0:T(8,128)} %param.12, bf16[16,1024,256]{2,1,0:T(8,128)(2,1)S(1)} %copy-done), kind=kLoop, calls=%fused_computation.2 | loop fusion | flops 16760832 | bytes 25231360 | tf_op jit(solution)/shard_map/reduce_sum | solution.py:15
  72.5 0.0 slice-done
  72.5 0.0 slice-done.1
  72.5 0.0 slice-done.4
  72.5 0.0 slice-done.2
  72.5 0.0 slice-done.3
  72.5 0.0 slice-done.5
  72.5 4.3 multiply_reduce_fusion.1
  76.9 0.0 all-reduce.3.cloned.1.call-update
  76.9 62.6 %all-reduce.3.cloned.1.call-done = (f32[16,1024]{1,0:T(8,128)}, f32[16,1024]{0,1:T(8,128)}, f32[16,1024]{0,1:T(8,128)}) async-done(((f32[16,1024]{1,0:T(8,128)}, f32[16,1024]{0,1:T(8,128)}, f32[16,1024]{0,1:T(8,128)}), (f32[16,1024]{1,0:T(8,128)}, f32[16,1024]{0,1:T(8,128)}, f32[16,1024]{0,1:T(8,128)})) %all-reduce.3.cloned.1.call-update) | async-done | bytes 196624 | tf_op jit(solution)/shard_map/psum | solution.py:11
  139.5 1.2 sqrt.10
  140.7 12.0 %divide_convert_fusion.1 = bf16[16,256,1024]{1,0,2:T(8,128)(2,1)} fusion(f32[16,256,1024]{1,0,2:T(8,128)} %copy.29, bf16[16,256,1024]{1,0,2:T(8,128)(2,1)} %copy.28, f32[16,1024]{0,1:T(8,128)S(1)} %sqrt.10), kind=kLoop, calls=%fused_computation.3 | loop fusion | flops 16777216 | bytes 33619968 | tf_op jit(solution)/shard_map/convert_element_type | solution.py:24
  152.7 0.0 copy-start.1
  152.7 5.3 all-to-all-start.1
  158.0 0.0 copy-done.1
  158.0 0.1 sqrt.11
  158.2 23.8 %divide_convert_fusion = bf16[16,1024,256]{2,0,1:T(8,128)(2,1)} fusion(f32[16,1024,256]{2,1,0:T(8,128)} %param.12, f32[16,1024]{0,1:T(8,128)S(1)} %sqrt.11, bf16[16,1024,256]{2,1,0:T(8,128)(2,1)} %param.13), kind=kLoop, calls=%fused_computation.1 | loop fusion | flops 16777216 | bytes 33619968 | tf_op jit(solution)/shard_map/convert_element_type | solution.py:25
  182.0 0.0 copy-start.2
  182.0 159.7 %all-to-all-done.1 = bf16[16,256,1024]{1,0,2:T(8,128)(2,1)} async-done(((bf16[16,256,1024]{1,0,2:T(8,128)(2,1)}), bf16[16,256,1024]{1,0,2:T(8,128)(2,1)}, u32[]{:S(2)}, u32[]{:S(2)}) %all-to-all-start.1) | async-done | bytes 8388640 | tf_op jit(solution)/shard_map/all_to_all | solution.py:34
  341.7 5.0 all-to-all-start.2
  346.7 0.0 copy-done.2
  346.7 9.4 %divide_convert_fusion.2 = bf16[16,256,1024]{2,1,0:T(8,128)(2,1)S(1)} fusion(f32[16,256,1024]{2,1,0:T(8,128)} %param.8, bf16[16,256,1024]{2,1,0:T(8,128)(2,1)} %param.9, f32[16,1024]{1,0:T(8,128)S(1)} %sqrt.9), kind=kLoop, calls=%fused_computation.6 | loop fusion | flops 16777216 | bytes 33619968 | tf_op jit(solution)/shard_map/convert_element_type | solution.py:23
  356.1 1.2 fusion.7
  357.4 1.2 fusion.6
  358.6 1.2 fusion.5
  359.9 1.2 fusion.4
  361.1 1.2 fusion.3
  362.4 1.2 fusion.2
  363.6 1.2 fusion.1
  364.8 1.2 fusion
  366.1 0.0 copy-start.3
  366.1 0.0 copy-start.4
  366.1 164.4 %all-to-all-done.2 = bf16[16,1024,256]{2,0,1:T(8,128)(2,1)} async-done(((bf16[16,1024,256]{2,0,1:T(8,128)(2,1)}), bf16[16,1024,256]{2,0,1:T(8,128)(2,1)}, u32[]{:S(2)}, u32[]{:S(2)}) %all-to-all-start.2) | async-done | bytes 8388640 | tf_op jit(solution)/shard_map/all_to_all | solution.py:36
  530.5 5.0 all-to-all-start
  535.5 0.0 copy-done.3
  535.5 0.0 copy-done.4
  535.5 189.9 %all_gather.6 = bf16[2048,16]{0,1:T(8,128)(2,1)S(1)} all-gather(bf16[256,16]{0,1:T(8,128)(2,1)S(1)} %multiply_convert_fusion), channel_id=1, replica_groups=mesh['owner'=4,'rows'=8] {'rows'}, dimensions={0}, use_global_device_ids=true | all-gather | bytes 73728 | tf_op jit(solution)/shard_map/all_gather | solution.py:47
  725.4 9.1 %all_gather.7 = bf16[2048,64]{0,1:T(8,128)(2,1)S(1)} all-gather(bf16[2048,16]{0,1:T(8,128)(2,1)S(1)} %all_gather.6), channel_id=1, replica_groups=mesh['owner'=4,'rows'=8] {'owner'}, dimensions={1}, use_global_device_ids=true | all-gather | bytes 327680 | tf_op jit(solution)/shard_map/all_gather | solution.py:48
  734.6 0.7 copy.35
  735.2 0.7 copy.34
  735.9 0.6 constant_dynamic-slice_fusion.2
  736.5 12.3 %copy.30 = bf16[16,8,256,128]{3,2,1,0:T(8,128)(2,1)} copy(bf16[16,8,256,128]{2,0,3,1:T(8,128)(2,1)} %bitcast.11) | data formatting | bytes 16777216 | tf_op jit(solution)/shard_map/all_to_all | solution.py:34
  748.8 11.4 %copy.33 = bf16[16,128,8,256]{3,2,1,0:T(8,128)(2,1)} copy(bf16[16,128,8,256]{3,0,1,2:T(8,128)(2,1)} %bitcast.14) | data formatting | bytes 16777216 | tf_op jit(solution)/shard_map/all_to_all | solution.py:36
  760.2 13.4 %all_to_all.37 = bf16[16,128,2048]{2,1,0:T(8,128)(2,1)} reshape(bf16[16,128,8,256]{3,2,1,0:T(8,128)(2,1)} %copy.33) | data formatting | bytes 16777216 | tf_op jit(solution)/shard_map/all_to_all | solution.py:36
  773.6 0.0 all-to-all-done
  773.6 7.9 copy.27
  781.5 0.7 copy.54
  (5 shorter events, 0.0 us)
Async XLA Ops:
  7.2 132.4 %all-reduce.3.cloned.1.call-start = ((), (), s32[]{:S(2)}) async-start(), calls=%async_computation.3 | async-start | bytes 2228224 | tf_op jit(solution)/shard_map/psum | solution.py:11
  37.3 10.7 %copy-start = (bf16[16,1024,256]{2,1,0:T(8,128)(2,1)S(1)}, bf16[16,1024,256]{2,1,0:T(8,128)(2,1)}, u32[]{:S(2)}) copy-start(bf16[16,1024,256]{2,1,0:T(8,128)(2,1)} %param.13) | copy-start | bytes 25165828
  37.3 35.2 %slice-start = ((s8[16777216]{0:T(1024)(128)(4,1)}), s8[4194304]{0:T(1024)(128)(4,1)S(1)}, s32[]{:S(2)}) async-start(s8[16777216]{0:T(1024)(128)(4,1)} %bitcast.43), calls=%async_computation.4 | async-start | bytes 8388608
  37.3 35.2 %slice-start.1 = ((s8[16777216]{0:T(1024)(128)(4,1)}), s8[4194304]{0:T(1024)(128)(4,1)S(1)}, s32[]{:S(2)}) async-start(s8[16777216]{0:T(1024)(128)(4,1)} %bitcast.43), calls=%async_computation.5 | async-start | bytes 8388608
  37.3 35.2 %slice-start.4 = ((s8[8388608]{0:T(1024)(128)(4,1)}), s8[4194304]{0:T(1024)(128)(4,1)S(1)}, s32[]{:S(2)}) async-start(s8[8388608]{0:T(1024)(128)(4,1)} %bitcast.45), calls=%async_computation.8 | async-start | bytes 8388608
  47.9 24.6 %slice-start.2 = ((s8[16777216]{0:T(1024)(128)(4,1)}), s8[4194304]{0:T(1024)(128)(4,1)S(1)}, s32[]{:S(2)}) async-start(s8[16777216]{0:T(1024)(128)(4,1)} %bitcast.43), calls=%async_computation.6 | async-start | bytes 8388608
  47.9 24.6 %slice-start.3 = ((s8[16777216]{0:T(1024)(128)(4,1)}), s8[4194304]{0:T(1024)(128)(4,1)S(1)}, s32[]{:S(2)}) async-start(s8[16777216]{0:T(1024)(128)(4,1)} %bitcast.43), calls=%async_computation.7 | async-start | bytes 8388608
  47.9 24.6 %slice-start.5 = ((s8[8388608]{0:T(1024)(128)(4,1)}), s8[4194304]{0:T(1024)(128)(4,1)S(1)}, s32[]{:S(2)}) async-start(s8[8388608]{0:T(1024)(128)(4,1)} %bitcast.45), calls=%async_computation.9 | async-start | bytes 8388608
  152.7 5.3 copy-start.1
  152.7 189.0 %all-to-all-start.1 = ((bf16[16,256,1024]{1,0,2:T(8,128)(2,1)}), bf16[16,256,1024]{1,0,2:T(8,128)(2,1)}, u32[]{:S(2)}, u32[]{:S(2)}) async-start(bf16[16,256,1024]{1,0,2:T(8,128)(2,1)} %divide_convert_fusion.1), calls=%async_computation.1 | async-start | bytes 16777216 | tf_op jit(solution)/shard_map/all_to_all | solution.py:34
  182.0 164.7 %copy-start.2 = (f32[16,1024]{1,0:T(8,128)S(1)}, f32[16,1024]{1,0:T(8,128)}, u32[]{:S(2)}) copy-start(f32[16,1024]{1,0:T(8,128)} %get-tuple-element.14) | copy-start | bytes 196612
  341.7 188.8 %all-to-all-start.2 = ((bf16[16,1024,256]{2,0,1:T(8,128)(2,1)}), bf16[16,1024,256]{2,0,1:T(8,128)(2,1)}, u32[]{:S(2)}, u32[]{:S(2)}) async-start(bf16[16,1024,256]{2,0,1:T(8,128)(2,1)} %divide_convert_fusion), calls=%async_computation.2 | async-start | bytes 16777216 | tf_op jit(solution)/shard_map/all_to_all | solution.py:36
  366.1 169.4 %copy-start.3 = (f32[256,16]{0,1:T(8,128)S(1)}, f32[256,16]{0,1:T(8,128)}, u32[]{:S(2)}) copy-start(f32[256,16]{0,1:T(8,128)} %param.14) | copy-start | bytes 49156
  366.1 169.4 %copy-start.4 = (f32[256]{0:T(256)S(1)}, f32[256]{0:T(256)}, u32[]{:S(2)}) copy-start(f32[256]{0:T(256)} %param.15) | copy-start | bytes 3076
  530.5 243.1 %all-to-all-start = ((bf16[8,16,256,128]{3,2,1,0:T(8,128)(2,1)}), bf16[8,16,256,128]{3,2,1,0:T(8,128)(2,1)}, u32[]{:S(2)}, u32[]{:S(2)}) async-start(bf16[8,16,256,128]{3,2,1,0:T(8,128)(2,1)} %fusion), calls=%async_computation | async-start | bytes 16777216 | tf_op jit(solution)/shard_map/all_to_all | solution.py:29
Sparse Core Ops, SparseCore 0:
  77.0 62.4 all-reduce.2
